TPU v7x, 32 devices: a whole 2x2x4 slice. The times are simulated.
32 devices in a mesh: seq: 8 (over z, y), head: 4 (over x, core).
Axes of the slice: x: 2, y: 2, z: 4, core: 2. Of those that a mesh axis runs over, the one named last changes fastest.
Arguments:
- query: bfloat16 [512, 2048], P('seq', 'head'), may hold values from -16 to 16
- key_states: bfloat16 [512, 2048], P('seq', 'head'), may hold values from -16 to 16
- value_states: bfloat16 [512, 2048], P('seq', 'head'), may hold values from -6 to 6
- doc_ids: int32 [512], P('seq'), may hold values from 0 to 3, never falling along the last dimension, each value on 1 to 256 neighbouring positions
- out_weight: bfloat16 [2048, 4096], P('head', 'seq'), may hold values from -0.1875 to 0.1875
- residual: bfloat16 [512, 4096], P('seq', 'head'), may hold values from -6 to 6
Outputs:
- mixed: bfloat16 [512, 4096], P('seq', 'head')
Inputs may be any that keep to these rules, and one draw needn't show every extreme that they name: doc_ids never fall along the sequence; every document has 1 to 256 positions, and one has exactly 256.
All inputs are finite; a program needn't handle non-finite values.
Results may differ from a plain program's by a relative error of at most 0.0055.
Values may be sent and summed in bfloat16 or wider, within the bound.
A program may use at most 64 MiB of HBM per device.

v0:
```python
import jax
import jax.numpy as jnp
from jax import lax
from jax.sharding import PartitionSpec as P

HEAD_DIM = 128
masked_score = -1e30


def to_heads(block):
    return block.reshape(block.shape[0], block.shape[1] // HEAD_DIM, HEAD_DIM)


def attend_block(state, queries, query_pos, query_docs, keys, values, key_pos, key_docs):
    run_max, run_sum, run_acc = state
    scores = jnp.einsum(
        "qhd,khd->hqk", queries, keys, preferred_element_type=jnp.float32
    ) * HEAD_DIM ** (-0.5)
    allowed = (key_pos[None, :] <= query_pos[:, None]) & (key_docs[None, :] == query_docs[:, None])
    scores = jnp.where(allowed[None], scores, masked_score)
    new_max = jnp.maximum(run_max, jnp.max(scores, axis=-1))
    weights = jnp.where(allowed[None], jnp.exp(scores - new_max[..., None]), 0.0)
    run_sum = jnp.sum(weights, axis=-1)
    run_acc = jnp.einsum(
        "hqk,khd->hqd", weights.astype(jnp.bfloat16), values, preferred_element_type=jnp.float32
    )
    return (new_max, run_sum, run_acc)


def shards(query, key_states, value_states, doc_ids, out_weight, residual):
    tok_rows = query.shape[0]
    heads = query.shape[1] // HEAD_DIM
    shard_index = lax.axis_index("seq")
    first_pos = shard_index * tok_rows
    groups = [(query, first_pos + jnp.arange(tok_rows, dtype=jnp.int32), doc_ids)]
    prepared = [(to_heads(block), block_pos, block_docs) for block, block_pos, block_docs in groups]
    initial = tuple(
        (
            (
                jnp.full((heads, block_pos.shape[0]), masked_score, jnp.float32),
                jnp.zeros((heads, block_pos.shape[0]), jnp.float32),
                jnp.zeros((heads, block_pos.shape[0], HEAD_DIM), jnp.float32),
            )
            for block, block_pos, block_docs in groups
        )
    )
    first_row = jnp.int32(0)
    keys = lax.all_gather(key_states, "seq", axis=0, tiled=True)
    values = lax.all_gather(value_states, "seq", axis=0, tiled=True)
    key_docs = lax.all_gather(doc_ids, "seq", axis=0, tiled=True)
    key_pos = jnp.arange(keys.shape[0], dtype=jnp.int32)
    key_heads = to_heads(keys)
    value_heads = to_heads(values)
    updated = []
    for member, state in zip(prepared, initial):
        queries, query_pos, query_docs = member

        def advance(inner, queries=queries, query_pos=query_pos, query_docs=query_docs):
            return attend_block(
                inner, queries, query_pos, query_docs, key_heads, value_heads, key_pos, key_docs
            )

        def unchanged(inner):
            return inner

        updated.append(lax.cond(first_row <= jnp.max(query_pos), advance, unchanged, state))
    finals = tuple(updated)
    outputs = []
    for run_max, run_sum, run_acc in finals:
        normed = run_acc / run_sum[..., None]
        outputs.append(
            jnp.transpose(normed, (1, 0, 2))
            .reshape(normed.shape[1], heads * HEAD_DIM)
            .astype(jnp.bfloat16)
        )
    attended = outputs[0]
    mapped = jnp.dot(
        attended,
        lax.all_gather(out_weight, "seq", axis=1, tiled=True),
        preferred_element_type=jnp.float32,
    )
    summed = lax.psum_scatter(mapped, "head", scatter_dimension=1, tiled=True)
    return (residual.astype(jnp.float32) + summed).astype(jnp.bfloat16)


def solution(mesh):
    placed = (
        P("seq", "head"),
        P("seq", "head"),
        P("seq", "head"),
        P("seq"),
        P("head", "seq"),
        P("seq", "head"),
    )
    return jax.shard_map(
        shards, mesh=mesh, in_specs=placed, out_specs=P("seq", "head"), check_vma=False
    )
```

profile of v0, /device:TPU:0, one launch (start us, length us, event | category | flops | bytes accessed | tf_op | source)
XLA Modules:
  0.0 137.0 jit_solution(2854361127337461728)
XLA Ops:
  6.5 0.0 all-gather.2.cloned.1.call-start
  6.5 0.7 all-gather.2.cloned.1.call-update
  7.3 0.0 reduce-scatter.2.cloned.1.call-start
  7.3 0.6 fusion.19
  8.6 1.3 dynamic-slice
  10.5 0.9 dynamic-update-slice
  11.3 13.2 %all-reduce = s32[512]{0:T(512)S(1)} all-reduce(s32[512]{0:T(512)S(1)} %dynamic-update-slice), channel_id=1, replica_groups=mesh['seq'=8,'head'=4] {'seq'}, use_global_device_ids=true, to_apply=%add | all-reduce | flops 512 | bytes 4096
  24.5 33.5 %all_gather.13 = bf16[512,512]{1,0:T(8,128)(2,1)S(1)} all-gather(bf16[64,512]{1,0:T(8,128)(2,1)} %param.9), channel_id=1, replica_groups=mesh['seq'=8,'head'=4] {'seq'}, dimensions={0}, use_global_device_ids=true | all-gather | bytes 589824 | tf_op jit(solution)/shard_map/all_gather | solution.py:48
  58.1 33.8 %all_gather.14 = bf16[512,512]{1,0:T(8,128)(2,1)S(1)} all-gather(bf16[64,512]{1,0:T(8,128)(2,1)} %param.10), channel_id=1, replica_groups=mesh['seq'=8,'head'=4] {'seq'}, dimensions={0}, use_global_device_ids=true | all-gather | bytes 589824 | tf_op jit(solution)/shard_map/all_gather | solution.py:49
  91.8 0.0 copy-start
  91.8 2.6 %conditional.1 = (f32[4,64]{1,0:T(4,128)S(1)}, f32[4,64,128]{2,1,0:T(8,128)S(1)}) conditional(s32[]{:T(128)} %convert_element_type.22, () %tuple.13, (s32[512]{0:T(512)S(1)}, s32[64]{0:T(128)S(1)}, s32[512]{0:T(512)S(1)}, s32[64]{0:T(128)}, bf16[64,512]{1,0:T(8,128)(2,1)}, /*index=5*/bf16[512,512]{1,0:T(8,128)(2,1)S(1)}, ...), branch_computations={%region_1.0_spmd, %region_2.5_spmd} | conditional | flops 68386560 | bytes 2959888 | solution.py:66
  91.8 0.8 compare_and_fusion
  92.6 1.2 fusion.20
  93.9 0.3 fusion.1
  94.2 0.2 fusion.7
  94.4 5.8 %all-gather.2.cloned.1.call-done = bf16[512,4096]{1,0:T(8,128)(2,1)} async-done(((bf16[512,512]{1,0:T(8,128)(2,1)}), bf16[512,4096]{1,0:T(8,128)(2,1)}) %all-gather.2.cloned.1.call-update) | async-done | bytes 4194320 | tf_op jit(solution)/shard_map/all_gather | solution.py:79
  100.2 4.1 %fusion.15 = f32[64,4096]{1,0:T(8,128)} fusion(bf16[512,4096]{1,0:T(8,128)(2,1)} %all-gather.2.cloned.1.call-done, f32[4,64,128]{2,1,0:T(8,128)S(1)} %get-tuple-element.31, f32[4,64]{1,0:T(4,128)S(1)} %get-tuple-element.32), kind=kOutput, calls=%fused_computation.20 | convolution fusion | flops 268500992 | bytes 5374976 | tf_op jit(solution)/shard_map/dot_general | solution.py:77
  104.2 0.0 reduce-scatter.2.cloned.1.call-update
  104.2 24.2 %reduce-scatter.2.cloned.1.call-done = f32[64,1024]{1,0:T(8,128)} async-done(((f32[64,4096]{1,0:T(8,128)}), f32[64,1024]{1,0:T(8,128)}) %reduce-scatter.2.cloned.1.call-update) | async-done | bytes 262160 | tf_op jit(solution)/shard_map/reduce_scatter | solution.py:82
  128.5 0.0 copy-done
  128.5 1.6 %add_convert_fusion = bf16[64,1024]{1,0:T(8,128)(2,1)} fusion(f32[64,1024]{1,0:T(8,128)} %reduce-scatter.2.cloned.1.call-done, bf16[64,1024]{1,0:T(8,128)(2,1)S(1)} %copy-done), kind=kLoop, calls=%fused_computation.18 | loop fusion | flops 196608 | bytes 524288 | tf_op jit(solution)/shard_map/convert_element_type | solution.py:83
  (4 shorter events, 0.0 us)
Async XLA Ops:
  6.5 93.6 %all-gather.2.cloned.1.call-start = ((), (), s32[]{:S(2)}) async-start(), calls=%async_computation.1 | async-start | bytes 4718592 | tf_op jit(solution)/shard_map/all_gather | solution.py:79
  7.3 121.2 %reduce-scatter.2.cloned.1.call-start = ((), (), s32[]{:S(2)}) async-start(), calls=%async_computation.2 | async-start | bytes 1310720 | tf_op jit(solution)/shard_map/reduce_scatter | solution.py:82
  91.8 36.7 %copy-start = (bf16[64,1024]{1,0:T(8,128)(2,1)S(1)}, bf16[64,1024]{1,0:T(8,128)(2,1)}, u32[]{:S(2)}) copy-start(bf16[64,1024]{1,0:T(8,128)(2,1)} %param.13) | copy-start | bytes 393220
Sparse Core Ops, SparseCore 0:
  9.4 90.7 all-gather.1
  104.4 24.0 reduce-scatter.1
where the time goes:
time: 137 us
  blocking collectives  80.5 us (59%)
  waiting for transfers between devices  30.7 us (22%)
  between operations  14.7 us (11%)
  matrix products  5.57 us (4%)
  other arithmetic  3.29 us (2%)
  local copies, waits for them, and re-layouts  2.12 us (2%)
    all_gather x1, blocking collectives, shards(): values = lax.all_gather(value_states, 'seq', axis=0, tiled=True)  33.8 us
    all_gather x1, blocking collectives, shards(): keys = lax.all_gather(key_states, 'seq', axis=0, tiled=True)  33.5 us
    reduce_scatter x1, waiting for transfers between devices, shards(): summed = lax.psum_scatter(mapped, 'head', scatter_dimension=1, tiled=True)  24.2 us
    unnamed x1, blocking collectives  13.2 us
    all_gather x1, waiting for transfers between devices, shards(): lax.all_gather(out_weight, 'seq', axis=1, tiled=True)  5.75 us
    dot_general x1, matrix products, shards(): jnp.dot(attended, lax.all_gather(out_weight, 'seq', axis=1, tiled=True),...  4.06 us
  transfers between devices with their start and end apart: 2, of which 2 were waited for; matrix products, arithmetic and copies ran while one was open for 4% of the time, Pallas kernels for 0%

commit v1 on v0

--- a/solution.py
+++ b/solution.py
@@ -5,6 +5,12 @@
 
 HEAD_DIM = 128
 masked_score = -1e30
+
+
+def joined_along(blocks, dim):
+    blocks = jnp.moveaxis(blocks, 0, dim)
+    lengths = blocks.shape
+    return blocks.reshape(*lengths[:dim], lengths[dim] * lengths[dim + 1], *lengths[dim + 2 :])
 
 
 def to_heads(block):
@@ -46,7 +52,14 @@
     )
     first_row = jnp.int32(0)
     keys = lax.all_gather(key_states, "seq", axis=0, tiled=True)
-    values = lax.all_gather(value_states, "seq", axis=0, tiled=True)
+    length = lax.axis_size("seq")
+    ahead = [(i, (i + 1) % length) for i in range(length)]
+    tiles = [value_states]
+    while len(tiles) < length:
+        tiles.append(lax.ppermute(tiles[-1], "seq", ahead))
+    position = lax.axis_index("seq")
+    tiles = jnp.stack(tiles)[(position - jnp.arange(length)) % length]
+    values = joined_along(tiles, 0)
     key_docs = lax.all_gather(doc_ids, "seq", axis=0, tiled=True)
     key_pos = jnp.arange(keys.shape[0], dtype=jnp.int32)
     key_heads = to_heads(keys)

time: 137 us -> 146 us (1.066)
  waiting for transfers between devices: 30.7 us -> 68.3 us
  blocking collectives: 80.5 us -> 47.3 us
  starting transfers between devices: 0.04 us -> 3.16 us
  local copies, waits for them, and re-layouts: 2.12 us -> 3.69 us
    ppermute x0 -> x7, waiting for transfers between devices: none -> 45.4 us  [shards(): tiles.append(lax.ppermute(tiles[-1], 'seq', ahead))]
    all_gather x1 -> x0, blocking collectives: 33.8 us -> none  [shards(): values = lax.all_gather(value_states, 'seq', axis=0, tiled=True)]
    all_gather x1, waiting for transfers between devices: 5.75 us -> 0.02 us  [shards(): lax.all_gather(out_weight, 'seq', axis=1, tiled=True)]
    ppermute x0 -> x7, starting transfers between devices: none -> 3.12 us  [shards(): tiles.append(lax.ppermute(tiles[-1], 'seq', ahead))]
    reduce_scatter x1, waiting for transfers between devices: 24.2 us -> 22.2 us  [shards(): summed = lax.psum_scatter(mapped, 'head', scatter_dimension=1, tiled=True)]
    unnamed x5 -> x12, local copies, waits for them, and re-layouts: 2.11 us -> 2.98 us
  transfers between devices with their start and end apart: 2 -> 9, of which waited for: 2 -> 7; matrix products, arithmetic and copies ran while one was open for 4% -> 5% of each run, Pallas kernels for 0% -> 0%
where the time goes in v1:
time: 146 us
  waiting for transfers between devices  68.3 us (47%)
  blocking collectives  47.3 us (32%)
  between operations  14.7 us (10%)
  matrix products  5.61 us (4%)
  local copies, waits for them, and re-layouts  3.69 us (3%)
  other arithmetic  3.29 us (2%)
  starting transfers between devices  3.16 us (2%)
    ppermute x7, waiting for transfers between devices, shards(): tiles.append(lax.ppermute(tiles[-1], 'seq', ahead))  45.4 us
    all_gather x1, blocking collectives, shards(): keys = lax.all_gather(key_states, 'seq', axis=0, tiled=True)  33.6 us
    reduce_scatter x1, waiting for transfers between devices, shards(): summed = lax.psum_scatter(mapped, 'head', scatter_dimension=1, tiled=True)  22.2 us
    unnamed x1, blocking collectives  13.7 us
    dot_general x1, matrix products, shards(): jnp.dot(attended, lax.all_gather(out_weight, 'seq', axis=1, tiled=True),...  4.09 us
    ppermute x7, starting transfers between devices, shards(): tiles.append(lax.ppermute(tiles[-1], 'seq', ahead))  3.12 us
    unnamed x12, local copies, waits for them, and re-layouts  2.98 us
  transfers between devices with their start and end apart: 9, of which 7 were waited for; matrix products, arithmetic and copies ran while one was open for 5% of the time, Pallas kernels for 0%

profile of v1, /device:TPU:0, one launch (start us, length us, event | category | flops | bytes accessed | tf_op | source)
XLA Modules:
  0.0 146.2 jit_solution(6923606614684664150)
XLA Ops:
  6.5 0.0 all-gather.2.cloned.1.call-start
  6.5 0.7 all-gather.2.cloned.1.call-update
  7.3 0.0 reduce-scatter.2.cloned.1.call-start
  7.3 3.0 %collective-permute-start = (bf16[64,512]{1,0:T(8,128)(2,1)}, bf16[64,512]{1,0:T(8,128)(2,1)S(1)}, u32[]{:S(2)}, u32[]{:S(2)}) collective-permute-start(bf16[64,512]{1,0:T(8,128)(2,1)} %param.10), channel_id=1, source_target_pairs={{0,4},{4,8},{8,12},{12,16},{16,20},{20,24},{24,28},{28,0},{1,5},{5... | collective-permute-start | bytes 196616 | tf_op jit(solution)/shard_map/ppermute | solution.py:59
  10.3 0.6 fusion.22
  11.6 1.2 dynamic-slice
  13.5 0.9 dynamic-update-slice
  14.3 13.7 %all-reduce = s32[512]{0:T(512)S(1)} all-reduce(s32[512]{0:T(512)S(1)} %dynamic-update-slice), channel_id=1, replica_groups=mesh['seq'=8,'head'=4] {'seq'}, use_global_device_ids=true, to_apply=%add | all-reduce | flops 512 | bytes 4096
  28.0 0.8 bitcast_dynamic-update-slice_fusion.7
  28.9 33.6 %all_gather.10 = bf16[512,512]{1,0:T(8,128)(2,1)S(1)} all-gather(bf16[64,512]{1,0:T(8,128)(2,1)} %param.9), channel_id=1, replica_groups=mesh['seq'=8,'head'=4] {'seq'}, dimensions={0}, use_global_device_ids=true | all-gather | bytes 589824 | tf_op jit(solution)/shard_map/all_gather | solution.py:54
  62.5 0.0 collective-permute-done
  62.5 0.1 collective-permute-start.1
  62.6 7.0 %collective-permute-done.1 = bf16[64,512]{1,0:T(8,128)(2,1)S(1)} collective-permute-done((bf16[64,512]{1,0:T(8,128)(2,1)S(1)}, bf16[64,512]{1,0:T(8,128)(2,1)S(1)}, u32[]{:S(2)}, u32[]{:S(2)}) %collective-permute-start.1) | collective-permute-done | bytes 65568 | tf_op jit(solution)/shard_map/ppermute | solution.py:59
  69.6 0.0 collective-permute-start.2
  69.7 8.5 %collective-permute-done.2 = bf16[64,512]{1,0:T(8,128)(2,1)S(1)} collective-permute-done((bf16[64,512]{1,0:T(8,128)(2,1)S(1)}, bf16[64,512]{1,0:T(8,128)(2,1)S(1)}, u32[]{:S(2)}, u32[]{:S(2)}) %collective-permute-start.2) | collective-permute-done | bytes 65568 | tf_op jit(solution)/shard_map/ppermute | solution.py:59
  78.1 0.0 collective-permute-start.3
  78.1 7.1 %collective-permute-done.3 = bf16[64,512]{1,0:T(8,128)(2,1)S(1)} collective-permute-done((bf16[64,512]{1,0:T(8,128)(2,1)S(1)}, bf16[64,512]{1,0:T(8,128)(2,1)S(1)}, u32[]{:S(2)}, u32[]{:S(2)}) %collective-permute-start.3) | collective-permute-done | bytes 65568 | tf_op jit(solution)/shard_map/ppermute | solution.py:59
  85.3 0.0 collective-permute-start.4
  85.3 8.8 %collective-permute-done.4 = bf16[64,512]{1,0:T(8,128)(2,1)S(1)} collective-permute-done((bf16[64,512]{1,0:T(8,128)(2,1)S(1)}, bf16[64,512]{1,0:T(8,128)(2,1)S(1)}, u32[]{:S(2)}, u32[]{:S(2)}) %collective-permute-start.4) | collective-permute-done | bytes 65568 | tf_op jit(solution)/shard_map/ppermute | solution.py:59
  94.1 0.0 collective-permute-start.5
  94.1 7.0 %collective-permute-done.5 = bf16[64,512]{1,0:T(8,128)(2,1)S(1)} collective-permute-done((bf16[64,512]{1,0:T(8,128)(2,1)S(1)}, bf16[64,512]{1,0:T(8,128)(2,1)S(1)}, u32[]{:S(2)}, u32[]{:S(2)}) %collective-permute-start.5) | collective-permute-done | bytes 65568 | tf_op jit(solution)/shard_map/ppermute | solution.py:59
  101.1 0.0 collective-permute-start.6
  101.1 7.0 %collective-permute-done.6 = bf16[64,512]{1,0:T(8,128)(2,1)S(1)} collective-permute-done((bf16[64,512]{1,0:T(8,128)(2,1)S(1)}, bf16[64,512]{1,0:T(8,128)(2,1)S(1)}, u32[]{:S(2)}, u32[]{:S(2)}) %collective-permute-start.6) | collective-permute-done | bytes 65568 | tf_op jit(solution)/shard_map/ppermute | solution.py:59
  108.0 3.3 %conditional.1 = (f32[4,64]{1,0:T(4,128)S(1)}, f32[4,64,128]{2,1,0:T(8,128)S(1)}) conditional(s32[]{:T(128)} %convert_element_type.22, () %tuple.13, (s32[512]{0:T(512)S(1)}, s32[64]{0:T(128)S(1)}, s32[512]{0:T(512)S(1)}, s32[64]{0:T(128)}, bf16[64,512]{1,0:T(8,128)(2,1)}, /*index=5*/bf16[512,512]{1,0:T(8,128)(2,1)S(1)}, ...), branch_computations={%region_1.2_spmd, %region_2.5_spmd.clone.clone} | conditional | flops 68387664 | bytes 5061336 | solution.py:79
  108.1 0.8 compare_and_fusion
  108.8 1.2 fusion.23
  110.1 0.6 gather_fusion
  110.7 0.1 reshape_reshape.5
  110.8 0.3 fusion.3
  111.1 0.2 fusion.6
  111.3 0.0 copy-start
  111.4 0.0 all-gather.2.cloned.1.call-done
  111.4 4.1 %fusion.16 = f32[64,4096]{1,0:T(8,128)} fusion(bf16[512,4096]{1,0:T(8,128)(2,1)} %all-gather.2.cloned.1.call-done, f32[4,64,128]{2,1,0:T(8,128)S(1)} %get-tuple-element.45, f32[4,64]{1,0:T(4,128)S(1)} %get-tuple-element.46), kind=kOutput, calls=%fused_computation.26 | convolution fusion | flops 268500992 | bytes 5374976 | tf_op jit(solution)/shard_map/dot_general | solution.py:90
  115.5 0.0 reduce-scatter.2.cloned.1.call-update
  115.5 22.2 %reduce-scatter.2.cloned.1.call-done = f32[64,1024]{1,0:T(8,128)} async-done(((f32[64,4096]{1,0:T(8,128)}), f32[64,1024]{1,0:T(8,128)}) %reduce-scatter.2.cloned.1.call-update) | async-done | bytes 262160 | tf_op jit(solution)/shard_map/reduce_scatter | solution.py:95
  137.7 0.0 copy-done
  137.7 1.6 %add_convert_fusion = bf16[64,1024]{1,0:T(8,128)(2,1)} fusion(f32[64,1024]{1,0:T(8,128)} %reduce-scatter.2.cloned.1.call-done, bf16[64,1024]{1,0:T(8,128)(2,1)S(1)} %copy-done), kind=kLoop, calls=%fused_computation.24 | loop fusion | flops 196608 | bytes 524288 | tf_op jit(solution)/shard_map/convert_element_type | solution.py:96
  (16 shorter events, 0.1 us)
Async XLA Ops:
  6.5 104.8 %all-gather.2.cloned.1.call-start = ((), (), s32[]{:S(2)}) async-start(), calls=%async_computation.1 | async-start | bytes 4718592 | tf_op jit(solution)/shard_map/all_gather | solution.py:92
  7.3 130.5 %reduce-scatter.2.cloned.1.call-start = ((), (), s32[]{:S(2)}) async-start(), calls=%async_computation.2 | async-start | bytes 1310720 | tf_op jit(solution)/shard_map/reduce_scatter | solution.py:95
  7.3 55.2 %collective-permute-start = (bf16[64,512]{1,0:T(8,128)(2,1)}, bf16[64,512]{1,0:T(8,128)(2,1)S(1)}, u32[]{:S(2)}, u32[]{:S(2)}) collective-permute-start(bf16[64,512]{1,0:T(8,128)(2,1)} %param.10), channel_id=1, source_target_pairs={{0,4},{4,8},{8,12},{12,16},{16,20},{20,24},{24,28},{28,0},{1,5},{5... | collective-permute-start | bytes 196616 | tf_op jit(solution)/shard_map/ppermute | solution.py:59
  62.5 7.1 %collective-permute-start.1 = (bf16[64,512]{1,0:T(8,128)(2,1)S(1)}, bf16[64,512]{1,0:T(8,128)(2,1)S(1)}, u32[]{:S(2)}, u32[]{:S(2)}) collective-permute-start(bf16[64,512]{1,0:T(8,128)(2,1)S(1)} %collective-permute-done), channel_id=1, source_target_pairs={{0,4},{4,8},{8,12},{12,16},{16,20},{20,24},{24,28},{28,0},{1,5},{5... | collective-permute-start | bytes 196616 | tf_op jit(solution)/shard_map/ppermute | solution.py:59
  69.6 8.5 %collective-permute-start.2 = (bf16[64,512]{1,0:T(8,128)(2,1)S(1)}, bf16[64,512]{1,0:T(8,128)(2,1)S(1)}, u32[]{:S(2)}, u32[]{:S(2)}) collective-permute-start(bf16[64,512]{1,0:T(8,128)(2,1)S(1)} %collective-permute-done.1), channel_id=1, source_target_pairs={{0,4},{4,8},{8,12},{12,16},{16,20},{20,24},{24,28},{28,0},{1,5},{5... | collective-permute-start | bytes 196616 | tf_op jit(solution)/shard_map/ppermute | solution.py:59
  78.1 7.1 %collective-permute-start.3 = (bf16[64,512]{1,0:T(8,128)(2,1)S(1)}, bf16[64,512]{1,0:T(8,128)(2,1)S(1)}, u32[]{:S(2)}, u32[]{:S(2)}) collective-permute-start(bf16[64,512]{1,0:T(8,128)(2,1)S(1)} %collective-permute-done.2), channel_id=1, source_target_pairs={{0,4},{4,8},{8,12},{12,16},{16,20},{20,24},{24,28},{28,0},{1,5},{5... | collective-permute-start | bytes 196616 | tf_op jit(solution)/shard_map/ppermute | solution.py:59
  85.3 8.8 %collective-permute-start.4 = (bf16[64,512]{1,0:T(8,128)(2,1)S(1)}, bf16[64,512]{1,0:T(8,128)(2,1)S(1)}, u32[]{:S(2)}, u32[]{:S(2)}) collective-permute-start(bf16[64,512]{1,0:T(8,128)(2,1)S(1)} %collective-permute-done.3), channel_id=1, source_target_pairs={{0,4},{4,8},{8,12},{12,16},{16,20},{20,24},{24,28},{28,0},{1,5},{5... | collective-permute-start | bytes 196616 | tf_op jit(solution)/shard_map/ppermute | solution.py:59
  94.1 7.0 %collective-permute-start.5 = (bf16[64,512]{1,0:T(8,128)(2,1)S(1)}, bf16[64,512]{1,0:T(8,128)(2,1)S(1)}, u32[]{:S(2)}, u32[]{:S(2)}) collective-permute-start(bf16[64,512]{1,0:T(8,128)(2,1)S(1)} %collective-permute-done.4), channel_id=1, source_target_pairs={{0,4},{4,8},{8,12},{12,16},{16,20},{20,24},{24,28},{28,0},{1,5},{5... | collective-permute-start | bytes 196616 | tf_op jit(solution)/shard_map/ppermute | solution.py:59
  101.1 7.0 %collective-permute-start.6 = (bf16[64,512]{1,0:T(8,128)(2,1)S(1)}, bf16[64,512]{1,0:T(8,128)(2,1)S(1)}, u32[]{:S(2)}, u32[]{:S(2)}) collective-permute-start(bf16[64,512]{1,0:T(8,128)(2,1)S(1)} %collective-permute-done.5), channel_id=1, source_target_pairs={{0,4},{4,8},{8,12},{12,16},{16,20},{20,24},{24,28},{28,0},{1,5},{5... | collective-permute-start | bytes 196616 | tf_op jit(solution)/shard_map/ppermute | solution.py:59
  111.3 26.4 %copy-start = (bf16[64,1024]{1,0:T(8,128)(2,1)S(1)}, bf16[64,1024]{1,0:T(8,128)(2,1)}, u32[]{:S(2)}) copy-start(bf16[64,1024]{1,0:T(8,128)(2,1)} %param.13) | copy-start | bytes 393220
Sparse Core Ops, SparseCore 0:
  9.4 84.8 all-gather.1
  115.6 22.0 reduce-scatter.1
